TPU v7x, 32 devices: a whole 2x2x4 slice. The times are simulated.
32 devices in a mesh: parts: 2 (over x), dp: 16 (over z, y, core).
Axes of the slice: x: 2, y: 2, z: 4, core: 2. Of those that a mesh axis runs over, the one named last changes fastest.
Arguments:
- activations: bfloat16 [8192, 14336], P(('parts', 'dp')), parts along dimension 0, may hold values from -6 to 6
- out_grads: bfloat16 [8192, 4096], P(('parts', 'dp')), parts along dimension 0, may hold values from -6 to 6
- lengths: int32 [32, 4], P(('parts', 'dp')), parts along dimension 0, may hold values from 1 to 128, 256 in all within a row
- proj_in: bfloat16 [14336, 64], replicated, may hold values from -0.046875 to 0.046875
- proj_out: bfloat16 [4096, 64], replicated, may hold values from -0.09375 to 0.09375
- queries: bfloat16 [1024, 4096], P(('parts', 'dp')), parts along dimension 0, may hold values from -0.01171875 to 0.01171875
Outputs:
- scores: bfloat16 [128, 512], P(('parts', 'dp')), parts along dimension 0
There are 2 independent parts, one for each index of `parts`. A program takes and returns all parts, laid end to end along the dimension named above; an argument that names none is the same for every part. Nothing has to cross between parts.
Inputs may be any that keep to these rules, and one draw needn't show every extreme that they name: Each row of lengths sums to 256, and one entry of each row equals 128.
All inputs are finite; a program needn't handle non-finite values.
Results may differ from a plain program's by a relative error of at most 0.0065.
Values may be sent and summed in bfloat16 or wider, within the bound.
A program may use at most 128 MiB of HBM per device.

v0:
```python
import jax
import jax.numpy as jnp
from jax import lax
from jax.sharding import PartitionSpec as P


def local(activations, out_grads, lengths, proj_in, proj_out, queries):
    tok_count = activations.shape[0]
    rank_size = proj_in.shape[1]
    proj_acts = jnp.dot(activations, proj_in, preferred_element_type=jnp.float32).astype(
        jnp.bfloat16
    )
    proj_grads = jnp.dot(out_grads, proj_out, preferred_element_type=jnp.float32).astype(
        jnp.bfloat16
    )
    counts = lengths[0]
    tok_ends = jnp.cumsum(counts)
    tok_starts = tok_ends - counts
    position = jnp.arange(tok_count, dtype=jnp.int32)
    member = (
        (position[None, :] >= tok_starts[:, None]) & (position[None, :] < tok_ends[:, None])
    ).astype(jnp.bfloat16)
    masked_grads = member[:, :, None] * proj_grads[None, :, :]
    summed = jnp.einsum("eti,tj->eij", masked_grads, proj_acts, preferred_element_type=jnp.float32)
    example_grads = summed.reshape(counts.shape[0], rank_size * rank_size).astype(jnp.bfloat16)
    contract = (((1,), (1,)), ((), ()))
    local_scores = lax.dot_general(
        lax.all_gather(example_grads, "dp", axis=0, tiled=True),
        queries,
        contract,
        preferred_element_type=jnp.float32,
    ).astype(jnp.bfloat16)
    return lax.all_to_all(local_scores, "dp", split_axis=0, concat_axis=1, tiled=True)


def solution(mesh):
    in_specs = (
        P(("parts", "dp"), None),
        P(("parts", "dp"), None),
        P(("parts", "dp"), None),
        P(),
        P(),
        P(("parts", "dp"), None),
    )
    out_specs = P(("parts", "dp"), None)
    return jax.shard_map(local, mesh=mesh, in_specs=in_specs, out_specs=out_specs, check_vma=False)
```

profile of v0, /device:TPU:0, one launch (start us, length us, event | category | flops | bytes accessed | tf_op | source)
XLA Modules:
  0.0 44.8 jit_solution(8421804942782179360)
XLA Ops:
  0.0 0.0 copy-start
  0.0 1.0 %reduce-window.7 = s32[4,1]{0,1:T(1,128)S(1)} reduce-window(s32[4,1]{0,1:T(1,128)} %bitcast.20, s32[]{:T(128)} %constant.3.clone.1), window={size=4x1 pad=3_0x0_0}, to_apply=%region_0.0 | reduce-window | flops 12 | bytes 36 | tf_op jit(solution)/shard_map/reduce-window.2
  1.0 0.7 %bitcast_subtract_fusion = s32[4]{0:T(128)S(1)} fusion(s32[1,4]{1,0:T(1,128)} %param.8, s32[4,1]{0,1:T(1,128)S(1)} %reduce-window.7), kind=kLoop, calls=%fused_computation.12 | loop fusion | flops 4 | bytes 48 | tf_op jit(solution)/shard_map/sub | solution.py:18
  1.6 0.1 fusion.5
  1.7 0.0 copy-done
  1.7 1.8 %convolution_convert_fusion.2 = bf16[256,64]{0,1:T(8,128)(2,1)S(1)} fusion(bf16[256,4096]{1,0:T(8,128)(2,1)S(1)} %copy-done, bf16[4096,64]{0,1:T(8,128)(2,1)} %param.10), kind=kOutput, calls=%fused_computation.2 | convolution fusion | flops 134234112 | bytes 2654208 | tf_op jit(solution)/shard_map/dot_general | solution.py:13
  3.5 0.0 copy-start.1
  3.5 6.2 %convolution_convert_fusion = bf16[4,64,64]{2,1,0:T(8,128)(2,1)S(1)} fusion(bf16[256,14336]{1,0:T(8,128)(2,1)} %param.6, bf16[14336,64]{0,1:T(8,128)(2,1)} %param.9, bf16[256,64]{0,1:T(8,128)(2,1)S(1)} %convolution_convert_fusion.2, bf16[4,256]{1,0:T(4,128)(2,1)S(1)} %fusion.5), kind=kOutput, calls=%fused_computation | convolution fusion | flops 478248960 | bytes 9242624 | tf_op jit(solution)/shard_map/eti,tj->eij/dot_general | solution.py:24
  9.7 0.1 reshape.80
  9.9 24.6 %all-gather = bf16[16,4,4096]{2,1,0:T(4,128)(2,1)S(1)} all-gather(bf16[1,4,4096]{2,1,0:T(4,128)(2,1)S(1)} %reshape.80), channel_id=1, replica_groups=mesh['parts'=2,'dp'=16] {'dp'}, dimensions={0}, use_global_device_ids=true | all-gather | bytes 557056 | tf_op jit(solution)/shard_map/all_gather | solution.py:28
  34.5 0.1 reshape.81
  34.6 0.0 copy-done.1
  34.6 0.3 convolution_convert_fusion.3
  34.9 0.1 copy.11
  35.0 9.1 %all_to_all.19 = bf16[16,4,32]{2,1,0:T(4,128)(2,1)S(1)} all-to-all(bf16[16,4,32]{2,1,0:T(4,128)(2,1)S(1)} %bitcast.17), channel_id=1, replica_groups=mesh['parts'=2,'dp'=16] {'dp'}, dimensions={0} | all-to-all | bytes 8192 | tf_op jit(solution)/shard_map/all_to_all | solution.py:33
  44.1 0.7 %all_to_all.17 = bf16[4,512]{1,0:T(4,128)(2,1)} reshape(bf16[4,16,32]{2,1,0:T(8,128)(2,1)S(1)} %copy.12) | data formatting | bytes 8192 | tf_op jit(solution)/shard_map/all_to_all | solution.py:33
  (1 shorter events, 0.0 us)
Async XLA Ops:
  0.0 1.7 %copy-start = (bf16[256,4096]{1,0:T(8,128)(2,1)S(1)}, bf16[256,4096]{1,0:T(8,128)(2,1)}, u32[]{:S(2)}) copy-start(bf16[256,4096]{1,0:T(8,128)(2,1)} %param.7) | copy-start | bytes 6291460
  3.5 31.1 %copy-start.1 = (bf16[32,4096]{1,0:T(8,128)(2,1)S(1)}, bf16[32,4096]{1,0:T(8,128)(2,1)}, u32[]{:S(2)}) copy-start(bf16[32,4096]{1,0:T(8,128)(2,1)} %param.11) | copy-start | bytes 786436
where the time goes:
time: 45 us; the launch traced here: 44.8 us
  blocking collectives  33.7 us (75%)
  matrix products  8.27 us (18%)
  other arithmetic  1.71 us (4%)
  local copies, waits for them, and re-layouts  1.04 us (2%)
    all_gather x1, blocking collectives, local(): lax.all_gather(example_grads, 'dp', axis=0, tiled=True)  24.6 us
    all_to_all x1, blocking collectives, local(): lax.all_to_all(local_scores, 'dp', split_axis=0, concat_axis=1, tiled=True)  9.07 us
    dot_general x1, matrix products, local(): jnp.einsum('eti,tj->eij', masked_grads, proj_acts, preferred_element_type...  6.21 us
    dot_general x1, matrix products, local(): jnp.dot(out_grads, proj_out, preferred_element_type=jnp.float32)  1.8 us
    another operation x1, other arithmetic  0.97 us

commit v1 on v0

--- a/solution.py
+++ b/solution.py
@@ -30,7 +30,10 @@
         contract,
         preferred_element_type=jnp.float32,
     ).astype(jnp.bfloat16)
-    return lax.all_to_all(local_scores, "dp", split_axis=0, concat_axis=1, tiled=True)
+    return jnp.concatenate(
+        lax.all_to_all(jnp.stack(jnp.split(local_scores, lax.axis_size("dp"), axis=0)), "dp", 0, 0),
+        axis=1,
+    )
 
 
 def solution(mesh):

time: 45 us -> 46.7 us (1.038)
  local copies, waits for them, and re-layouts: 1.04 us -> 2.68 us
    split x0 -> x17, local copies, waits for them, and re-layouts: none -> 1.61 us  [local(): jnp.split(local_scores, lax.axis_size('dp'), axis=0)]
    all_to_all x2 -> x0, local copies, waits for them, and re-layouts: 0.69 us -> none  [local(): lax.all_to_all(local_scores, 'dp', split_axis=0, concat_axis=1, tiled=True)]
    reshape x0 -> x2, local copies, waits for them, and re-layouts: none -> 0.69 us  [local(): jnp.concatenate(lax.all_to_all(jnp.stack(jnp.split(local_scores, lax.axis...]
where the time goes in v1:
time: 46.7 us; the launch traced here: 46.5 us
  blocking collectives  33.7 us (72%)
  matrix products  8.27 us (18%)
  local copies, waits for them, and re-layouts  2.68 us (6%)
  other arithmetic  1.71 us (4%)
    all_gather x1, blocking collectives, local(): lax.all_gather(example_grads, 'dp', axis=0, tiled=True)  24.6 us
    all_to_all x1, blocking collectives, local(): lax.all_to_all(jnp.stack(jnp.split(local_scores, lax.axis_size('dp'), axi...  9.07 us
    dot_general x1, matrix products, local(): jnp.einsum('eti,tj->eij', masked_grads, proj_acts, preferred_element_type...  6.21 us
    dot_general x1, matrix products, local(): jnp.dot(out_grads, proj_out, preferred_element_type=jnp.float32)  1.8 us
    split x17, local copies, waits for them, and re-layouts, local(): jnp.split(local_scores, lax.axis_size('dp'), axis=0)  1.61 us
    another operation x1, other arithmetic  0.97 us

profile of v1, /device:TPU:0, one launch (start us, length us, event | category | flops | bytes accessed | tf_op | source)
XLA Modules:
  0.0 46.5 jit_solution(14258477820824780418)
XLA Ops:
  0.0 0.0 copy-start
  0.0 1.0 %reduce-window.7 = s32[4,1]{0,1:T(1,128)S(1)} reduce-window(s32[4,1]{0,1:T(1,128)} %bitcast.50, s32[]{:T(128)} %constant.3.clone.1), window={size=4x1 pad=3_0x0_0}, to_apply=%region_0.0 | reduce-window | flops 12 | bytes 36 | tf_op jit(solution)/shard_map/reduce-window.2
  1.0 0.7 %bitcast_subtract_fusion = s32[4]{0:T(128)S(1)} fusion(s32[1,4]{1,0:T(1,128)} %param.8, s32[4,1]{0,1:T(1,128)S(1)} %reduce-window.7), kind=kLoop, calls=%fused_computation.28 | loop fusion | flops 4 | bytes 48 | tf_op jit(solution)/shard_map/sub | solution.py:18
  1.6 0.1 fusion.5
  1.7 0.0 copy-done
  1.7 1.8 %convolution_convert_fusion.2 = bf16[256,64]{0,1:T(8,128)(2,1)S(1)} fusion(bf16[256,4096]{1,0:T(8,128)(2,1)S(1)} %copy-done, bf16[4096,64]{0,1:T(8,128)(2,1)} %param.10), kind=kOutput, calls=%fused_computation.2 | convolution fusion | flops 134234112 | bytes 2654208 | tf_op jit(solution)/shard_map/dot_general | solution.py:13
  3.5 0.0 copy-start.1
  3.5 6.2 %convolution_convert_fusion = bf16[4,64,64]{2,1,0:T(8,128)(2,1)S(1)} fusion(bf16[256,14336]{1,0:T(8,128)(2,1)} %param.6, bf16[14336,64]{0,1:T(8,128)(2,1)} %param.9, bf16[256,64]{0,1:T(8,128)(2,1)S(1)} %convolution_convert_fusion.2, bf16[4,256]{1,0:T(4,128)(2,1)S(1)} %fusion.5), kind=kOutput, calls=%fused_computation | convolution fusion | flops 478248960 | bytes 9242624 | tf_op jit(solution)/shard_map/eti,tj->eij/dot_general | solution.py:24
  9.7 0.1 reshape.85
  9.9 24.6 %all-gather = bf16[16,4,4096]{2,1,0:T(4,128)(2,1)S(1)} all-gather(bf16[1,4,4096]{2,1,0:T(4,128)(2,1)S(1)} %reshape.85), channel_id=1, replica_groups=mesh['parts'=2,'dp'=16] {'dp'}, dimensions={0}, use_global_device_ids=true | all-gather | bytes 557056 | tf_op jit(solution)/shard_map/all_gather | solution.py:28
  34.5 0.1 reshape.86
  34.6 0.0 copy-done.1
  34.6 0.3 convolution_convert_fusion.3
  34.9 0.1 fusion.6
  35.0 0.1 copy.55
  35.1 0.1 copy.54
  35.2 0.1 copy.53
  35.3 0.1 copy.52
  35.4 0.1 copy.51
  35.5 0.1 copy.50
  35.5 0.1 copy.49
  35.6 0.1 copy.48
  35.7 0.1 copy.47
  35.8 0.1 copy.46
  35.9 0.1 copy.45
  36.0 0.1 copy.44
  36.1 0.1 copy.43
  36.2 0.1 copy.42
  36.3 0.1 copy.41
  36.4 0.1 copy.40
  36.7 9.1 %all_to_all.5 = bf16[16,4,32]{2,1,0:T(4,128)(2,1)S(1)} all-to-all(bf16[16,4,32]{2,1,0:T(4,128)(2,1)S(1)} %constant_dynamic-update-slice_fusion), channel_id=1, replica_groups=mesh['parts'=2,'dp'=16] {'dp'}, dimensions={0} | all-to-all | bytes 8192 | tf_op jit(solution)/shard_map/all_to_all | solution.py:34
  45.8 0.7 %reshape.84 = bf16[4,512]{1,0:T(4,128)(2,1)} reshape(bf16[4,16,32]{2,1,0:T(8,128)(2,1)S(1)} %copy.56) | data formatting | bytes 8192 | tf_op jit(solution)/shard_map/reshape | solution.py:33
  (17 shorter events, 0.1 us)
Async XLA Ops:
  0.0 1.7 %copy-start = (bf16[256,4096]{1,0:T(8,128)(2,1)S(1)}, bf16[256,4096]{1,0:T(8,128)(2,1)}, u32[]{:S(2)}) copy-start(bf16[256,4096]{1,0:T(8,128)(2,1)} %param.7) | copy-start | bytes 6291460
  3.5 31.1 %copy-start.1 = (bf16[32,4096]{1,0:T(8,128)(2,1)S(1)}, bf16[32,4096]{1,0:T(8,128)(2,1)}, u32[]{:S(2)}) copy-start(bf16[32,4096]{1,0:T(8,128)(2,1)} %param.11) | copy-start | bytes 786436
